TPU v7x, 32 devices: a whole 2x2x4 slice. The times are simulated.
32 devices in a mesh: rows: 8 (over z, x), ka: 4 (over y, core).
Axes of the slice: x: 2, y: 2, z: 4, core: 2. Of those that a mesh axis runs over, the one named last changes fastest.
Arguments:
- pair_repr: bfloat16 [512, 512, 128], P('rows', 'ka'), may hold values from -6 to 6
- pair_mask: int32 [512, 512], P('rows', 'ka'), may hold values 0 or 1
- ln_gain: float32 [128], replicated, may hold values from 0.1 to 1.9
- ln_bias: float32 [128], replicated, may hold values from -3 to 3
- w_proj: bfloat16 [128, 256], replicated, may hold values from -0.5 to 0.5
- w_gate: bfloat16 [128, 256], replicated, may hold values from -0.5 to 0.5
- w_out_gate: bfloat16 [128, 128], replicated, may hold values from -0.5 to 0.5
- out_gain: float32 [128], replicated, may hold values from 0.1 to 1.9
- out_bias: float32 [128], replicated, may hold values from -3 to 3
- w_out: bfloat16 [128, 128], replicated, may hold values from -0.5 to 0.5
Outputs:
- update: bfloat16 [512, 512, 128], P('rows', 'ka')
All inputs are finite; a program needn't handle non-finite values. No bound on the sum of `pair_mask` on one device may be relied on, other than what follows from the above.
Results may differ from a plain program's by a relative error of at most 0.015.
Values may be sent and summed in bfloat16 or wider, within the bound.
A program may use at most 64 MiB of HBM per device.

v0:
```python
import jax
import jax.numpy as jnp
from jax import lax
from jax.sharding import PartitionSpec as P


def layer_norm(values, gain_vec, bias_vec):
    center = jnp.mean(values, axis=-1, keepdims=True)
    deviate = values - center
    spread = jnp.mean(deviate * deviate, axis=-1, keepdims=True)
    return deviate * lax.rsqrt(spread + 1e-05) * gain_vec + bias_vec


def panel_sums(left_edge, right_edge):
    return jnp.einsum(
        "ikh,jkh->ijh",
        left_edge,
        lax.all_gather(right_edge, "rows", axis=0, tiled=True),
        preferred_element_type=jnp.float32,
    )


def body(
    pair_repr, pair_mask, ln_gain, ln_bias, w_proj, w_gate, w_out_gate, out_gain, out_bias, w_out
):
    row_count, col_count, chans = pair_repr.shape
    hidden = w_out.shape[0]
    normed = layer_norm(pair_repr.astype(jnp.float32), ln_gain, ln_bias).astype(jnp.bfloat16)
    flat_rows = normed.reshape(row_count * col_count, chans)
    projected = jnp.dot(flat_rows, w_proj, preferred_element_type=jnp.float32)
    gate_logits = jnp.dot(flat_rows, w_gate, preferred_element_type=jnp.float32)
    mask_col = pair_mask.reshape(row_count * col_count, 1).astype(jnp.float32)
    edges = (jax.nn.sigmoid(gate_logits) * projected * mask_col).astype(jnp.bfloat16)
    edges = edges.reshape(row_count, col_count, 2 * hidden)
    left_edge = edges[:, :, :hidden]
    right_edge = edges[:, :, hidden:]
    partial_sums = panel_sums(left_edge, right_edge)
    triangle = lax.psum_scatter(
        partial_sums.astype(jnp.bfloat16), "ka", scatter_dimension=1, tiled=True
    ).astype(jnp.float32)
    tri_normed = layer_norm(triangle, out_gain, out_bias).astype(jnp.bfloat16)
    out_gate = jax.nn.sigmoid(jnp.dot(flat_rows, w_out_gate, preferred_element_type=jnp.float32))
    projected_out = jnp.dot(
        tri_normed.reshape(row_count * col_count, hidden), w_out, preferred_element_type=jnp.float32
    )
    return (out_gate * projected_out).astype(jnp.bfloat16).reshape(row_count, col_count, chans)


def solution(mesh):
    placed = (P("rows", "ka", None), P("rows", "ka"), P(), P(), P(), P(), P(), P(), P(), P())
    return jax.shard_map(
        body, mesh=mesh, in_specs=placed, out_specs=P("rows", "ka", None), check_vma=False
    )
```

profile of v0, /device:TPU:17, one launch (start us, length us, event | category | flops | bytes accessed | tf_op | source)
XLA Modules:
  0.0 408.4 jit_solution(3869477217058959746)
XLA Ops:
  6.5 0.0 copy-start
  6.5 0.0 copy-start.2
  6.5 0.0 copy-start.8
  6.5 0.0 copy-start.10
  6.5 0.0 copy-start.9
  6.5 0.0 all-gather.2.cloned.1.call-start
  6.6 2.4 convert_reduce_fusion.1
  9.0 3.6 fusion.17
  12.6 0.0 copy-done.8
  12.6 0.0 copy-done.2
  12.6 0.0 copy-done.10
  12.6 0.0 copy-done.9
  12.6 2.5 fusion.20
  15.1 0.0 copy-start.3
  15.1 0.0 copy-done
  15.2 0.0 copy-start.6
  15.2 2.3 fusion.8
  17.5 0.0 copy-done.3
  17.5 0.0 copy-done.6
  17.5 3.6 fusion.3
  21.2 2.5 fusion.23
  23.7 2.9 copy.17
  26.6 0.0 all-gather.2.cloned.1.call-update
  26.6 0.2 reduce-scatter.4.cloned.1.call-start
  26.9 3.3 copy.18
  30.2 223.3 %all-gather.2.cloned.1.call-done = bf16[512,128,128]{1,0,2:T(8,128)(2,1)} async-done(((bf16[64,128,128]{1,0,2:T(8,128)(2,1)}), bf16[512,128,128]{1,0,2:T(8,128)(2,1)}) %all-gather.2.cloned.1.call-update) | async-done | bytes 16777232 | tf_op jit(solution)/shard_map/all_gather | solution.py:18
  253.5 11.4 %convert_bitcast_fusion = bf16[64,512,128]{1,0,2:T(8,128)(2,1)} fusion(bf16[512,128,128]{1,0,2:T(8,128)(2,1)} %all-gather.2.cloned.1.call-done, bf16[64,128,128]{1,0,2:T(8,128)(2,1)S(1)} %copy.18), kind=kOutput, calls=%fused_computation.13 | convolution fusion | flops 1077936128 | bytes 27262976 | tf_op jit(solution)/shard_map/ikh,jkh->ijh/dot_general | solution.py:15
  264.9 23.9 %copy.15 = bf16[64,512,128]{0,2,1:T(8,128)(2,1)} copy(bf16[64,512,128]{1,0,2:T(8,128)(2,1)} %convert_bitcast_fusion) | data formatting | bytes 16777216
  288.8 22.6 %reshape.53 = bf16[512,8192]{1,0:T(8,128)(2,1)} reshape(bf16[512,128,64]{2,1,0:T(8,128)(2,1)} %bitcast.25) | data formatting | bytes 16777216
  311.4 0.0 copy-start.4
  311.4 0.0 copy-start.13
  311.4 0.0 reduce-scatter.4.cloned.1.call-update
  311.4 1.6 copy-done.4
  313.0 0.0 copy-done.13
  313.0 3.2 fusion.7
  316.2 66.5 %reduce-scatter.4.cloned.1.call-done = bf16[128,8192]{1,0:T(8,128)(2,1)} async-done(((bf16[512,8192]{1,0:T(8,128)(2,1)}), bf16[128,8192]{1,0:T(8,128)(2,1)}) %reduce-scatter.4.cloned.1.call-update) | async-done | bytes 2097168
  382.6 6.9 %reshape.54 = bf16[128,128,64]{2,1,0:T(8,128)(2,1)} reshape(bf16[128,8192]{1,0:T(8,128)(2,1)} %reduce-scatter.4.cloned.1.call-done) | data formatting | bytes 4194304
  389.6 0.0 copy-start.11
  389.6 0.0 copy-start.12
  389.6 5.9 %copy.16 = bf16[64,128,128]{1,0,2:T(8,128)(2,1)S(1)} copy(bf16[64,128,128]{0,2,1:T(8,128)(2,1)} %bitcast.30) | data formatting | bytes 4194304
  395.5 0.0 copy-start.5
  395.5 0.0 copy-start.7
  395.5 0.4 convert_reduce_fusion
  395.8 0.6 fusion.13
  396.5 0.0 copy-done.11
  396.5 0.0 copy-done.12
  396.5 0.9 fusion.16
  397.3 0.0 copy-start.1
  397.4 0.3 copy-done.5
  397.6 0.0 copy-done.7
  397.6 3.9 fusion.6
  401.6 0.0 copy-done.1
  (5 shorter events, 0.0 us)
Async XLA Ops:
  6.5 8.6 %copy-start = (bf16[128,256]{1,0:T(8,128)(2,1)S(1)}, bf16[128,256]{1,0:T(8,128)(2,1)}, u32[]{:S(2)}) copy-start(bf16[128,256]{1,0:T(8,128)(2,1)} %param.15) | copy-start | bytes 196612
  6.5 6.1 %copy-start.2 = (bf16[64,128,128]{2,1,0:T(8,128)(2,1)S(1)}, bf16[64,128,128]{2,1,0:T(8,128)(2,1)}, u32[]{:S(2)}) copy-start(bf16[64,128,128]{2,1,0:T(8,128)(2,1)} %param.10) | copy-start | bytes 6291460
  6.5 6.0 %copy-start.8 = (s32[64,128]{1,0:T(8,128)S(1)}, s32[64,128]{1,0:T(8,128)}, u32[]{:S(2)}) copy-start(s32[64,128]{1,0:T(8,128)} %param.11) | copy-start | bytes 98308
  6.5 6.1 %copy-start.10 = (f32[128]{0:T(128)S(1)}, f32[128]{0:T(128)}, u32[]{:S(2)}) copy-start(f32[128]{0:T(128)} %param.12) | copy-start | bytes 1540
  6.5 6.1 %copy-start.9 = (f32[128]{0:T(128)S(1)}, f32[128]{0:T(128)}, u32[]{:S(2)}) copy-start(f32[128]{0:T(128)} %param.13) | copy-start | bytes 1540
  6.5 246.9 %all-gather.2.cloned.1.call-start = ((), (), s32[]{:S(2)}) async-start(), calls=%async_computation.1 | async-start | bytes 18874368 | tf_op jit(solution)/shard_map/all_gather | solution.py:18
  15.1 2.4 copy-start.3
  15.2 2.4 copy-start.6
  26.6 356.0 %reduce-scatter.4.cloned.1.call-start = ((), (), s32[]{:S(2)}) async-start(), calls=%async_computation.2 | async-start | bytes 10485760
  311.4 1.6 copy-start.4
  311.4 1.6 copy-start.13
  389.6 6.9 %copy-start.11 = (f32[128]{0:T(128)S(1)}, f32[128]{0:T(128)}, u32[]{:S(2)}) copy-start(f32[128]{0:T(128)} %param.18) | copy-start | bytes 1540
  389.6 6.9 %copy-start.12 = (f32[128]{0:T(128)S(1)}, f32[128]{0:T(128)}, u32[]{:S(2)}) copy-start(f32[128]{0:T(128)} %param.17) | copy-start | bytes 1540
  395.5 2.2 copy-start.5
  395.5 2.2 copy-start.7
  397.3 4.2 %copy-start.1 = (bf16[128,256]{1,0:T(8,128)(2,1)S(1)}, bf16[128,256]{1,0:T(8,128)(2,1)}, u32[]{:S(2)}) copy-start(bf16[128,256]{1,0:T(8,128)(2,1)} %param.15) | copy-start | bytes 196612
Sparse Core Ops, SparseCore 0:
  26.7 226.6 all-gather.1
  311.5 71.0 reduce-scatter.3
where the time goes:
time: 412 us; the launch traced here: 408 us
  waiting for transfers between devices  290 us (70%)
  local copies, waits for them, and re-layouts  69.9 us (17%)
  matrix products  24.5 us (6%)
  between operations  13.6 us (3%)
  other arithmetic  10.3 us (2%)
    all_gather x1, waiting for transfers between devices, panel_sums(): lax.all_gather(right_edge, 'rows', axis=0, tiled=True)  223 us
    unnamed x34, local copies, waits for them, and re-layouts  67.4 us
    unnamed x3, waiting for transfers between devices  66.5 us
    dot_general x1, matrix products, panel_sums(): jnp.einsum('ikh,jkh->ijh', left_edge, lax.all_gather(right_edge, 'rows',...  11.4 us
  transfers between devices with their start and end apart: 2, of which 2 were waited for; matrix products, arithmetic and copies ran while one was open for 2% of the time, Pallas kernels for 0%

commit v1 on v0

v1 whole, which is shorter than its diff:
```python
import functools

import jax
import jax.numpy as jnp
from jax import lax
from jax.experimental import pallas as pl
from jax.experimental.pallas import tpu as pltpu
from jax.sharding import PartitionSpec as P

MESH = pl.DeviceIdType.MESH
CHUNK = 16


def layer_norm(values, gain_vec, bias_vec):
    center = jnp.mean(values, axis=-1, keepdims=True)
    deviate = values - center
    spread = jnp.mean(deviate * deviate, axis=-1, keepdims=True)
    return deviate * lax.rsqrt(spread + 1e-05) * gain_vec + bias_vec


def sigmoid(logits):
    return 0.5 + 0.5 * jnp.tanh(0.5 * logits)


def kernel(
    rows_n, ka_n, halves,
    pair_ref, mask_ref, ln_gain_ref, ln_bias_ref, w_proj_ref, w_gate_ref, w_out_gate_ref,
    out_gain_ref, out_bias_ref, w_out_ref,
    out_ref,
    edges, wide, normed, gates, left, right, tri, back, w_cat, gain_col, bias_col,
    recv_lr, send_left, send_right, recv_tri, send_tri,
):
    row = lax.axis_index("rows")
    col = lax.axis_index("ka")
    row_count, col_count, chans = pair_ref.shape
    hidden = w_out_ref.shape[0]
    group_rows = rows_n // halves
    members = group_rows * ka_n
    share = hidden // members
    half = row // group_rows
    spot = row % group_rows
    member = spot * ka_n + col
    chunks = row_count // CHUNK

    barrier = pltpu.get_barrier_semaphore()

    def greet(step, carry):
        to_row = (row + step // ka_n) % rows_n
        to_col = (col + step % ka_n) % ka_n
        pl.semaphore_signal(barrier, inc=1, device_id=(to_row, to_col), device_id_type=MESH)
        return carry

    lax.fori_loop(1, rows_n * ka_n, greet, 0)

    def turned(ref):
        return ref[...].astype(jnp.float32).T.astype(jnp.bfloat16)

    w_cat[: 2 * hidden, :] = turned(w_gate_ref)
    w_cat[2 * hidden :, :] = turned(w_proj_ref)
    gain_col[...] = jnp.broadcast_to(out_gain_ref[...], (col_count, hidden)).T
    bias_col[...] = jnp.broadcast_to(out_bias_ref[...], (col_count, hidden)).T

    def left_copy(chunk, to_spot, to_col):
        to_member = to_spot * ka_n + to_col
        return pltpu.make_async_remote_copy(
            src_ref=edges.at[pl.ds(to_member * share, share), pl.ds(chunk * CHUNK, CHUNK), :],
            dst_ref=left.at[
                :, pl.ds(spot * row_count + chunk * CHUNK, CHUNK), pl.ds(pl.multiple_of(col * col_count, 128), col_count)
            ],
            send_sem=send_left,
            recv_sem=recv_lr.at[0],
            device_id=(half * group_rows + to_spot, to_col),
            device_id_type=MESH,
        )

    def right_copy(chunk, turn, to_spot, to_col):
        to_member = to_spot * ka_n + to_col
        to_half = (half + turn) % halves
        return pltpu.make_async_remote_copy(
            src_ref=edges.at[
                pl.ds(hidden + to_member * share, share), pl.ds(chunk * CHUNK, CHUNK), :
            ],
            dst_ref=right.at[
                :, pl.ds(row * row_count + chunk * CHUNK, CHUNK), pl.ds(pl.multiple_of(col * col_count, 128), col_count)
            ],
            send_sem=send_right.at[turn],
            recv_sem=recv_lr.at[1],
            device_id=(to_half * group_rows + to_spot, to_col),
            device_id_type=MESH,
        )

    def partner(step):
        return (spot + step // ka_n) % group_rows, (col + step % ka_n) % ka_n

    def make_chunk(chunk):
        def one_row(local, carry):
            at = chunk * CHUNK + local
            values = pair_ref[at].astype(jnp.float32)
            plain = layer_norm(values, ln_gain_ref[...], ln_bias_ref[...]).astype(jnp.bfloat16)
            normed[at] = plain
            both = lax.dot_general(
                w_cat[...], plain, (((1,), (1,)), ((), ())), preferred_element_type=jnp.float32
            )
            mask_row = mask_ref[pl.ds(at, 1), :].astype(jnp.float32)
            made = sigmoid(both[: 2 * hidden]) * both[2 * hidden :] * mask_row
            wide[pl.ds(local, 2 * hidden, stride=CHUNK), :] = made
            return carry

        lax.fori_loop(0, CHUNK, one_row, 0, unroll=2)
        packed = wide[...].reshape(2 * hidden, CHUNK, col_count).astype(jnp.bfloat16)
        edges[:, pl.ds(pl.multiple_of(chunk * CHUNK, CHUNK), CHUNK), :] = packed

    def send_chunk(chunk):
        def far(step, carry):
            for turn in range(1, halves):
                right_copy(chunk, turn, *partner(step)).start()
            return carry

        lax.fori_loop(0, members, far, 0)

        def near(step, carry):
            to_spot, to_col = partner(step)
            left_copy(chunk, to_spot, to_col).start()
            right_copy(chunk, 0, to_spot, to_col).start()
            return carry

        lax.fori_loop(1, members, near, 0)

    make_chunk(0)
    pl.semaphore_wait(barrier, rows_n * ka_n - 1)
    send_chunk(0)

    def rest(chunk, carry):
        make_chunk(chunk)
        send_chunk(chunk)
        return carry

    lax.fori_loop(1, chunks, rest, 0)

    own_cols = pl.ds(pl.multiple_of(col * col_count, 128), col_count)
    pltpu.make_async_copy(
        edges.at[pl.ds(member * share, share)],
        left.at[:, pl.ds(spot * row_count, row_count), own_cols],
        recv_lr.at[0],
    ).start()
    pltpu.make_async_copy(
        edges.at[pl.ds(hidden + member * share, share)],
        right.at[:, pl.ds(row * row_count, row_count), own_cols],
        recv_lr.at[1],
    ).start()

    def gate_row(at, carry):
        gates[at] = sigmoid(
            jnp.dot(normed[at], w_out_gate_ref[...], preferred_element_type=jnp.float32)
        )
        return carry

    lax.fori_loop(0, row_count, gate_row, 0, unroll=2)

    pltpu.make_async_copy(left, left, recv_lr.at[0]).wait()
    pltpu.make_async_copy(right, right, recv_lr.at[1]).wait()

    def tri_src(chan, to_spot, to_col):
        return tri.at[
            chan, pl.ds(to_spot * row_count, row_count), pl.ds(pl.multiple_of(to_col * col_count, 128), col_count)
        ]

    def one_channel(chan, carry):
        tri[chan] = lax.dot_general(
            left[chan], right[chan], (((1,), (1,)), ((), ())), preferred_element_type=jnp.float32
        ).astype(jnp.bfloat16)
        slot = back.at[member * share + chan]

        def give(step, inner):
            to_spot, to_col = partner(step)
            pltpu.make_async_remote_copy(
                src_ref=tri_src(chan, to_spot, to_col),
                dst_ref=slot,
                send_sem=send_tri,
                recv_sem=recv_tri,
                device_id=(half * group_rows + to_spot, to_col),
                device_id_type=MESH,
            ).start()
            return inner

        lax.fori_loop(1, members, give, 0)
        pltpu.make_async_copy(tri_src(chan, spot, col), slot, recv_tri).start()
        return carry

    lax.fori_loop(0, share, one_channel, 0)

    pltpu.make_async_copy(back, back, recv_tri).wait()

    def finish(chunk, carry):
        first = pl.multiple_of(chunk * CHUNK, CHUNK)
        sums = back[:, pl.ds(first, CHUNK), :].astype(jnp.float32)
        center = jnp.mean(sums, axis=0, keepdims=True)
        deviate = sums - center
        spread = jnp.mean(deviate * deviate, axis=0, keepdims=True)
        scaled = deviate * lax.rsqrt(spread + 1e-05)
        wide[: hidden * CHUNK, :] = scaled.reshape(hidden * CHUNK, col_count)

        def one_row(local, inner):
            at = first + local
            chans_first = wide[pl.ds(local, hidden, stride=CHUNK), :]
            tri_normed = (chans_first * gain_col[...] + bias_col[...]).astype(jnp.bfloat16)
            projected = lax.dot_general(
                tri_normed, w_out_ref[...], (((0,), (0,)), ((), ())), preferred_element_type=jnp.float32
            )
            out_ref[at] = (gates[at] * projected).astype(jnp.bfloat16)
            return inner

        lax.fori_loop(0, CHUNK, one_row, 0, unroll=2)
        return carry

    lax.fori_loop(0, chunks, finish, 0)

    others = pl.ds(0, (members - 1) * share)
    pltpu.make_async_copy(edges.at[others], edges.at[others], send_left).wait()
    pltpu.make_async_copy(edges.at[others], edges.at[others], send_right.at[0]).wait()
    for turn in range(1, halves):
        every = pl.ds(0, hidden)
        pltpu.make_async_copy(edges.at[every], edges.at[every], send_right.at[turn]).wait()
    pltpu.make_async_copy(back.at[others], back.at[others], send_tri).wait()


def fused(rows_n, ka_n, halves, args):
    pair_repr, pair_mask, ln_gain, ln_bias, w_proj, w_gate, w_out_gate, out_gain, out_bias, w_out = args
    row_count, col_count, chans = pair_repr.shape
    hidden = w_out.shape[0]
    members = rows_n // halves * ka_n
    share = hidden // members
    half = jnp.bfloat16
    return pl.pallas_call(
        functools.partial(kernel, rows_n, ka_n, halves),
        out_shape=jax.ShapeDtypeStruct(pair_repr.shape, half),
        in_specs=[pl.BlockSpec(memory_space=pltpu.VMEM)] * 10,
        out_specs=pl.BlockSpec(memory_space=pltpu.VMEM),
        scratch_shapes=[
            pltpu.VMEM((2 * hidden, row_count, col_count), half),
            pltpu.VMEM((2 * hidden * CHUNK, col_count), jnp.float32),
            pltpu.VMEM((row_count, col_count, chans), half),
            pltpu.VMEM((row_count, col_count, chans), jnp.float32),
            pltpu.VMEM((share, rows_n // halves * row_count, ka_n * col_count), half),
            pltpu.VMEM((share, rows_n * row_count, ka_n * col_count), half),
            pltpu.VMEM((share, rows_n // halves * row_count, ka_n * col_count), half),
            pltpu.VMEM((hidden, row_count, col_count), half),
            pltpu.VMEM((4 * hidden, chans), half),
            pltpu.VMEM((hidden, col_count), jnp.float32),
            pltpu.VMEM((hidden, col_count), jnp.float32),
            pltpu.SemaphoreType.DMA((2,)),
            pltpu.SemaphoreType.DMA,
            pltpu.SemaphoreType.DMA((halves,)),
            pltpu.SemaphoreType.DMA,
            pltpu.SemaphoreType.DMA,
        ],
        compiler_params=pltpu.CompilerParams(
            collective_id=0, has_side_effects=True, vmem_limit_bytes=60 * 2**20
        ),
    )(
        pair_repr, pair_mask, ln_gain[None], ln_bias[None], w_proj, w_gate, w_out_gate,
        out_gain[None], out_bias[None], w_out,
    )


def plain(args):
    pair_repr, pair_mask, ln_gain, ln_bias, w_proj, w_gate, w_out_gate, out_gain, out_bias, w_out = args
    row_count, col_count, chans = pair_repr.shape
    hidden = w_out.shape[0]
    normed = layer_norm(pair_repr.astype(jnp.float32), ln_gain, ln_bias).astype(jnp.bfloat16)
    flat_rows = normed.reshape(row_count * col_count, chans)
    projected = jnp.dot(flat_rows, w_proj, preferred_element_type=jnp.float32)
    gate_logits = jnp.dot(flat_rows, w_gate, preferred_element_type=jnp.float32)
    mask_col = pair_mask.reshape(row_count * col_count, 1).astype(jnp.float32)
    edges = (jax.nn.sigmoid(gate_logits) * projected * mask_col).astype(jnp.bfloat16)
    edges = edges.reshape(row_count, col_count, 2 * hidden)
    partial_sums = jnp.einsum(
        "ikh,jkh->ijh",
        edges[:, :, :hidden],
        lax.all_gather(edges[:, :, hidden:], "rows", axis=0, tiled=True),
        preferred_element_type=jnp.float32,
    )
    triangle = lax.psum_scatter(
        partial_sums.astype(jnp.bfloat16), "ka", scatter_dimension=1, tiled=True
    ).astype(jnp.float32)
    tri_normed = layer_norm(triangle, out_gain, out_bias).astype(jnp.bfloat16)
    out_gate = jax.nn.sigmoid(jnp.dot(flat_rows, w_out_gate, preferred_element_type=jnp.float32))
    projected_out = jnp.dot(
        tri_normed.reshape(row_count * col_count, hidden), w_out, preferred_element_type=jnp.float32
    )
    return (out_gate * projected_out).astype(jnp.bfloat16).reshape(row_count, col_count, chans)


def body(rows_n, ka_n, *args):
    row_count, col_count, chans = args[0].shape
    hidden = args[-1].shape[0]
    halves = 2 if rows_n % 2 == 0 else 1
    members = rows_n // halves * ka_n
    aligned = row_count % CHUNK == 0 and col_count % 128 == 0 and chans % 128 == 0 and hidden % 128 == 0
    if aligned and hidden % members == 0 and col_count == hidden:
        return fused(rows_n, ka_n, halves, args)
    return plain(args)


def solution(mesh):
    placed = (P("rows", "ka", None), P("rows", "ka"), P(), P(), P(), P(), P(), P(), P(), P())
    return jax.shard_map(
        functools.partial(body, mesh.shape["rows"], mesh.shape["ka"]),
        mesh=mesh, in_specs=placed, out_specs=P("rows", "ka", None), check_vma=False,
    )
```

time: 412 us -> 150 us (0.36)
  waiting for transfers between devices: 290 us -> 0 us
  Pallas kernels: 0 us -> 144 us
  local copies, waits for them, and re-layouts: 69.9 us -> 3.16 us
  matrix products: 24.5 us -> 0 us
  between operations: 13.6 us -> 0.01 us
  other arithmetic: 10.3 us -> 0 us
    all_gather x1 -> x0, waiting for transfers between devices: 223 us -> none  [panel_sums(): lax.all_gather(right_edge, 'rows', axis=0, tiled=True)]
    pallas_call x0 -> x1, Pallas kernels: none -> 144 us  [fused(): pl.pallas_call(functools.partial(kernel, rows_n, ka_n, halves), out_shape...]
    unnamed x3 -> x0, waiting for transfers between devices: 66.5 us -> none
    unnamed x34 -> x1, local copies, waits for them, and re-layouts: 67.4 us -> 3.16 us
    dot_general x5 -> x0, matrix products: 24.5 us -> none  [the longest x1 11.4 us: panel_sums(): jnp.einsum('ikh,jkh->ijh', left_edge, lax.all_gather(right_edge, 'rows',...]
    reduce_sum x4 -> x0, other arithmetic: 6.89 us -> none  [the longest x2 4.17 us: layer_norm(): spread = jnp.mean(deviate * deviate, axis=-1, keepdims=True)]
  transfers between devices with their start and end apart: 2 -> 0, of which waited for: 2 -> 0; matrix products, arithmetic and copies ran while one was open for 2% -> 0% of each run, Pallas kernels for 0% -> 0%
where the time goes in v1:
time: 150 us; the launch traced here: 148 us
  Pallas kernels  144 us (96%)
  local copies, waits for them, and re-layouts  3.16 us (2%)
    pallas_call x1, Pallas kernels, fused(): pl.pallas_call(functools.partial(kernel, rows_n, ka_n, halves), out_shape...  144 us
    unnamed x1, local copies, waits for them, and re-layouts  3.16 us

profile of v1, /device:TPU:17, one launch (start us, length us, event | category | flops | bytes accessed | tf_op | source)
XLA Modules:
  0.0 147.7 jit_solution(7649455468857276983)
XLA Ops:
  0.0 144.5 %shard_map.100 = bf16[64,128,128]{2,1,0:T(8,128)(2,1)} custom-call(bf16[64,128,128]{2,1,0:T(8,128)(2,1)} %pair_ref.1, s32[64,128]{1,0:T(8,128)} %mask_ref.1, f32[1,128]{1,0:T(1,128)} %bitcast.4, f32[1,128]{1,0:T(1,128)} %bitcast.5, bf16[128,256]{1,0:T(8,128)(2,1)} %w_proj_ref.1, bf16[128,256]{1,0:T(8,128)(2,1)} %w_gate_ref.1, ...), custom_call_target="tpu_custom_call" | custom-call | tf_op jit(solution)/shard_map/pallas_call | solution.py:234
  144.5 3.2 %copy.12 = bf16[64,128,128]{2,1,0:T(8,128)(2,1)} copy(bf16[64,128,128]{2,1,0:T(8,128)(2,1)} %shard_map.100) | data formatting | bytes 4194304

commit v2 on v1

--- a/solution.py
+++ b/solution.py
@@ -9,6 +9,7 @@
 
 MESH = pl.DeviceIdType.MESH
 CHUNK = 16
+PITCH = 24
 
 
 def layer_norm(values, gain_vec, bias_vec):
@@ -23,12 +24,12 @@
 
 
 def kernel(
-    rows_n, ka_n, halves,
-    pair_ref, mask_ref, ln_gain_ref, ln_bias_ref, w_proj_ref, w_gate_ref, w_out_gate_ref,
+    rows_n, ka_n, halves, groups,
+    pair_hbm, mask_ref, ln_gain_ref, ln_bias_ref, w_proj_ref, w_gate_ref, w_out_gate_ref,
     out_gain_ref, out_bias_ref, w_out_ref,
-    out_ref,
-    edges, wide, normed, gates, left, right, tri, back, w_cat, gain_col, bias_col,
-    recv_lr, send_left, send_right, recv_tri, send_tri,
+    out_hbm,
+    pair_ref, out_ref, edges, wide, normed, gates, left, right, tri, back, w_cat, gain_col, bias_col,
+    load_sem, store_sem, recv_left, recv_right, send_left, send_right, recv_tri, send_tri,
 ):
     row = lax.axis_index("rows")
     col = lax.axis_index("ka")
@@ -42,6 +43,19 @@
     member = spot * ka_n + col
     chunks = row_count // CHUNK
 
+    sub = share // groups
+    planes = wide.reshape(2 * hidden, PITCH, col_count)
+
+    def chunk_rows(chunk):
+        return pl.ds(pl.multiple_of(chunk * CHUNK, CHUNK), CHUNK)
+
+    def load(chunk):
+        rows = chunk_rows(chunk)
+        return pltpu.make_async_copy(pair_hbm.at[rows], pair_ref.at[rows], load_sem.at[chunk])
+
+    for chunk in range(chunks):
+        load(chunk).start()
+
     barrier = pltpu.get_barrier_semaphore()
 
     def greet(step, carry):
@@ -57,34 +71,30 @@
 
     w_cat[: 2 * hidden, :] = turned(w_gate_ref)
     w_cat[2 * hidden :, :] = turned(w_proj_ref)
-    gain_col[...] = jnp.broadcast_to(out_gain_ref[...], (col_count, hidden)).T
-    bias_col[...] = jnp.broadcast_to(out_bias_ref[...], (col_count, hidden)).T
-
-    def left_copy(chunk, to_spot, to_col):
+
+    own_cols = pl.ds(pl.multiple_of(col * col_count, 128), col_count)
+
+    def left_copy(group, first, size, to_spot, to_col):
         to_member = to_spot * ka_n + to_col
         return pltpu.make_async_remote_copy(
-            src_ref=edges.at[pl.ds(to_member * share, share), pl.ds(chunk * CHUNK, CHUNK), :],
-            dst_ref=left.at[
-                :, pl.ds(spot * row_count + chunk * CHUNK, CHUNK), pl.ds(pl.multiple_of(col * col_count, 128), col_count)
-            ],
+            src_ref=edges.at[pl.ds(to_member * share + group * sub, sub), pl.ds(first, size), :],
+            dst_ref=left.at[pl.ds(group * sub, sub), pl.ds(spot * row_count + first, size), own_cols],
             send_sem=send_left,
-            recv_sem=recv_lr.at[0],
+            recv_sem=recv_left.at[group],
             device_id=(half * group_rows + to_spot, to_col),
             device_id_type=MESH,
         )
 
-    def right_copy(chunk, turn, to_spot, to_col):
+    def right_copy(group, first, size, turn, to_spot, to_col):
         to_member = to_spot * ka_n + to_col
         to_half = (half + turn) % halves
         return pltpu.make_async_remote_copy(
             src_ref=edges.at[
-                pl.ds(hidden + to_member * share, share), pl.ds(chunk * CHUNK, CHUNK), :
+                pl.ds(hidden + to_member * share + group * sub, sub), pl.ds(first, size), :
             ],
-            dst_ref=right.at[
-                :, pl.ds(row * row_count + chunk * CHUNK, CHUNK), pl.ds(pl.multiple_of(col * col_count, 128), col_count)
-            ],
+            dst_ref=right.at[pl.ds(group * sub, sub), pl.ds(row * row_count + first, size), own_cols],
             send_sem=send_right.at[turn],
-            recv_sem=recv_lr.at[1],
+            recv_sem=recv_right.at[group],
             device_id=(to_half * group_rows + to_spot, to_col),
             device_id_type=MESH,
         )
@@ -93,6 +103,8 @@
         return (spot + step // ka_n) % group_rows, (col + step % ka_n) % ka_n
 
     def make_chunk(chunk):
+        load(chunk).wait()
+
         def one_row(local, carry):
             at = chunk * CHUNK + local
             values = pair_ref[at].astype(jnp.float32)
@@ -103,28 +115,30 @@
             )
             mask_row = mask_ref[pl.ds(at, 1), :].astype(jnp.float32)
             made = sigmoid(both[: 2 * hidden]) * both[2 * hidden :] * mask_row
-            wide[pl.ds(local, 2 * hidden, stride=CHUNK), :] = made
+            wide[pl.ds(local, 2 * hidden, stride=PITCH), :] = made
             return carry
 
         lax.fori_loop(0, CHUNK, one_row, 0, unroll=2)
-        packed = wide[...].reshape(2 * hidden, CHUNK, col_count).astype(jnp.bfloat16)
-        edges[:, pl.ds(pl.multiple_of(chunk * CHUNK, CHUNK), CHUNK), :] = packed
-
-    def send_chunk(chunk):
+        edges[:, chunk_rows(chunk), :] = planes[:, :CHUNK, :].astype(jnp.bfloat16)
+
+    def send_part(group, first, size):
         def far(step, carry):
             for turn in range(1, halves):
-                right_copy(chunk, turn, *partner(step)).start()
+                right_copy(group, first, size, turn, *partner(step)).start()
             return carry
 
         lax.fori_loop(0, members, far, 0)
 
         def near(step, carry):
             to_spot, to_col = partner(step)
-            left_copy(chunk, to_spot, to_col).start()
-            right_copy(chunk, 0, to_spot, to_col).start()
+            left_copy(group, first, size, to_spot, to_col).start()
+            right_copy(group, first, size, 0, to_spot, to_col).start()
             return carry
 
         lax.fori_loop(1, members, near, 0)
+
+    def send_chunk(chunk):
+        send_part(0, pl.multiple_of(chunk * CHUNK, CHUNK), CHUNK)
 
     make_chunk(0)
     pl.semaphore_wait(barrier, rows_n * ka_n - 1)
@@ -137,17 +151,24 @@
 
     lax.fori_loop(1, chunks, rest, 0)
 
-    own_cols = pl.ds(pl.multiple_of(col * col_count, 128), col_count)
-    pltpu.make_async_copy(
-        edges.at[pl.ds(member * share, share)],
-        left.at[:, pl.ds(spot * row_count, row_count), own_cols],
-        recv_lr.at[0],
-    ).start()
-    pltpu.make_async_copy(
-        edges.at[pl.ds(hidden + member * share, share)],
-        right.at[:, pl.ds(row * row_count, row_count), own_cols],
-        recv_lr.at[1],
-    ).start()
+    for group in range(1, groups):
+        send_part(group, 0, row_count)
+
+    for group in range(groups):
+        mine = pl.ds(group * sub, sub)
+        pltpu.make_async_copy(
+            edges.at[pl.ds(member * share + group * sub, sub)],
+            left.at[mine, pl.ds(spot * row_count, row_count), own_cols],
+            recv_left.at[group],
+        ).start()
+        pltpu.make_async_copy(
+            edges.at[pl.ds(hidden + member * share + group * sub, sub)],
+            right.at[mine, pl.ds(row * row_count, row_count), own_cols],
+            recv_right.at[group],
+        ).start()
+
+    gain_col[...] = jnp.broadcast_to(out_gain_ref[...], (col_count, hidden)).T
+    bias_col[...] = jnp.broadcast_to(out_bias_ref[...], (col_count, hidden)).T
 
     def gate_row(at, carry):
         gates[at] = sigmoid(
@@ -157,52 +178,62 @@
 
     lax.fori_loop(0, row_count, gate_row, 0, unroll=2)
 
-    pltpu.make_async_copy(left, left, recv_lr.at[0]).wait()
-    pltpu.make_async_copy(right, right, recv_lr.at[1]).wait()
-
-    def tri_src(chan, to_spot, to_col):
-        return tri.at[
-            chan, pl.ds(to_spot * row_count, row_count), pl.ds(pl.multiple_of(to_col * col_count, 128), col_count)
-        ]
-
     def one_channel(chan, carry):
         tri[chan] = lax.dot_general(
             left[chan], right[chan], (((1,), (1,)), ((), ())), preferred_element_type=jnp.float32
         ).astype(jnp.bfloat16)
-        slot = back.at[member * share + chan]
-
-        def give(step, inner):
-            to_spot, to_col = partner(step)
-            pltpu.make_async_remote_copy(
-                src_ref=tri_src(chan, to_spot, to_col),
-                dst_ref=slot,
-                send_sem=send_tri,
-                recv_sem=recv_tri,
-                device_id=(half * group_rows + to_spot, to_col),
-                device_id_type=MESH,
+        return carry
+
+    def tri_part(group, chunk, to_spot, to_col):
+        return tri.at[
+            pl.ds(group * sub, sub),
+            pl.ds(to_spot * row_count + chunk * CHUNK, CHUNK),
+            pl.ds(pl.multiple_of(to_col * col_count, 128), col_count),
+        ]
+
+    for group in range(groups):
+        mine = pl.ds(group * sub, sub)
+        pltpu.make_async_copy(left.at[mine], left.at[mine], recv_left.at[group]).wait()
+        pltpu.make_async_copy(right.at[mine], right.at[mine], recv_right.at[group]).wait()
+        lax.fori_loop(group * sub, (group + 1) * sub, one_channel, 0)
+
+        def give_chunk(chunk, carry):
+            slot = back.at[pl.ds(member * share + group * sub, sub), chunk_rows(chunk), :]
+
+            def give(step, inner):
+                to_spot, to_col = partner(step)
+                pltpu.make_async_remote_copy(
+                    src_ref=tri_part(group, chunk, to_spot, to_col),
+                    dst_ref=slot,
+                    send_sem=send_tri,
+                    recv_sem=recv_tri.at[chunk],
+                    device_id=(half * group_rows + to_spot, to_col),
+                    device_id_type=MESH,
+                ).start()
+                return inner
+
+            lax.fori_loop(1, members, give, 0)
+            pltpu.make_async_copy(
+                tri_part(group, chunk, spot, col), slot, recv_tri.at[chunk]
             ).start()
-            return inner
-
-        lax.fori_loop(1, members, give, 0)
-        pltpu.make_async_copy(tri_src(chan, spot, col), slot, recv_tri).start()
-        return carry
-
-    lax.fori_loop(0, share, one_channel, 0)
-
-    pltpu.make_async_copy(back, back, recv_tri).wait()
+            return carry
+
+        lax.fori_loop(0, chunks, give_chunk, 0)
 
     def finish(chunk, carry):
         first = pl.multiple_of(chunk * CHUNK, CHUNK)
+        arrived = back.at[:, chunk_rows(chunk), :]
+        pltpu.make_async_copy(arrived, arrived, recv_tri.at[chunk]).wait()
         sums = back[:, pl.ds(first, CHUNK), :].astype(jnp.float32)
         center = jnp.mean(sums, axis=0, keepdims=True)
         deviate = sums - center
         spread = jnp.mean(deviate * deviate, axis=0, keepdims=True)
         scaled = deviate * lax.rsqrt(spread + 1e-05)
-        wide[: hidden * CHUNK, :] = scaled.reshape(hidden * CHUNK, col_count)
+        planes[:hidden, :CHUNK, :] = scaled
 
         def one_row(local, inner):
             at = first + local
-            chans_first = wide[pl.ds(local, hidden, stride=CHUNK), :]
+            chans_first = wide[pl.ds(local, hidden, stride=PITCH), :]
             tri_normed = (chans_first * gain_col[...] + bias_col[...]).astype(jnp.bfloat16)
             projected = lax.dot_general(
                 tri_normed, w_out_ref[...], (((0,), (0,)), ((), ())), preferred_element_type=jnp.float32
@@ -211,9 +242,13 @@
             return inner
 
         lax.fori_loop(0, CHUNK, one_row, 0, unroll=2)
+        pltpu.make_async_copy(
+            out_ref.at[chunk_rows(chunk)], out_hbm.at[chunk_rows(chunk)], store_sem
+        ).start()
         return carry
 
     lax.fori_loop(0, chunks, finish, 0)
+    pltpu.make_async_copy(out_ref, out_hbm, store_sem).wait()
 
     others = pl.ds(0, (members - 1) * share)
     pltpu.make_async_copy(edges.at[others], edges.at[others], send_left).wait()
@@ -230,15 +265,18 @@
     hidden = w_out.shape[0]
     members = rows_n // halves * ka_n
     share = hidden // members
+    groups = 2 if share % 2 == 0 else 1
     half = jnp.bfloat16
     return pl.pallas_call(
-        functools.partial(kernel, rows_n, ka_n, halves),
+        functools.partial(kernel, rows_n, ka_n, halves, groups),
         out_shape=jax.ShapeDtypeStruct(pair_repr.shape, half),
-        in_specs=[pl.BlockSpec(memory_space=pltpu.VMEM)] * 10,
-        out_specs=pl.BlockSpec(memory_space=pltpu.VMEM),
+        in_specs=[pl.BlockSpec(memory_space=pl.ANY)] + [pl.BlockSpec(memory_space=pltpu.VMEM)] * 9,
+        out_specs=pl.BlockSpec(memory_space=pl.ANY),
         scratch_shapes=[
+            pltpu.VMEM((row_count, col_count, chans), half),
+            pltpu.VMEM((row_count, col_count, chans), half),
             pltpu.VMEM((2 * hidden, row_count, col_count), half),
-            pltpu.VMEM((2 * hidden * CHUNK, col_count), jnp.float32),
+            pltpu.VMEM((2 * hidden * PITCH, col_count), jnp.float32),
             pltpu.VMEM((row_count, col_count, chans), half),
             pltpu.VMEM((row_count, col_count, chans), jnp.float32),
             pltpu.VMEM((share, rows_n // halves * row_count, ka_n * col_count), half),
@@ -248,10 +286,13 @@
             pltpu.VMEM((4 * hidden, chans), half),
             pltpu.VMEM((hidden, col_count), jnp.float32),
             pltpu.VMEM((hidden, col_count), jnp.float32),
-            pltpu.SemaphoreType.DMA((2,)),
+            pltpu.SemaphoreType.DMA((row_count // CHUNK,)),
+            pltpu.SemaphoreType.DMA,
+            pltpu.SemaphoreType.DMA((groups,)),
+            pltpu.SemaphoreType.DMA((groups,)),
             pltpu.SemaphoreType.DMA,
             pltpu.SemaphoreType.DMA((halves,)),
-            pltpu.SemaphoreType.DMA,
+            pltpu.SemaphoreType.DMA((row_count // CHUNK,)),
             pltpu.SemaphoreType.DMA,
         ],
         compiler_params=pltpu.CompilerParams(

time: 150 us -> 139 us (0.927); the launches traced: 148 us -> 139 us
  Pallas kernels: 144 us -> 136 us
    pallas_call x1, Pallas kernels: 144 us -> 136 us  [fused(): pl.pallas_call(functools.partial(kernel, rows_n, ka_n, halves, groups), o...]
where the time goes in v2:
time: 139 us
  Pallas kernels  136 us (98%)
  local copies, waits for them, and re-layouts  3.16 us (2%)
    pallas_call x1, Pallas kernels, fused(): pl.pallas_call(functools.partial(kernel, rows_n, ka_n, halves, groups), o...  136 us
    unnamed x1, local copies, waits for them, and re-layouts  3.16 us

profile of v2, /device:TPU:17, one launch (start us, length us, event | category | flops | bytes accessed | tf_op | source)
XLA Modules:
  0.0 139.1 jit_solution(2722970638801961688)
XLA Ops:
  0.0 135.9 %shard_map.100 = bf16[64,128,128]{2,1,0:T(8,128)(2,1)} custom-call(bf16[64,128,128]{2,1,0:T(8,128)(2,1)} %pair_hbm.1, s32[64,128]{1,0:T(8,128)} %mask_ref.1, f32[1,128]{1,0:T(1,128)} %bitcast.4, f32[1,128]{1,0:T(1,128)} %bitcast.5, bf16[128,256]{1,0:T(8,128)(2,1)} %w_proj_ref.1, bf16[128,256]{1,0:T(8,128)(2,1)} %w_gate_ref.1, ...), custom_call_target="tpu_custom_call" | custom-call | tf_op jit(solution)/shard_map/pallas_call | solution.py:270
  136.0 3.2 %copy.12 = bf16[64,128,128]{2,1,0:T(8,128)(2,1)} copy(bf16[64,128,128]{2,1,0:T(8,128)(2,1)} %shard_map.100) | data formatting | bytes 4194304

commit v3 on v2

--- a/solution.py
+++ b/solution.py
@@ -100,7 +100,7 @@
         )
 
     def partner(step):
-        return (spot + step // ka_n) % group_rows, (col + step % ka_n) % ka_n
+        return (spot + step % group_rows) % group_rows, (col + step // group_rows) % ka_n
 
     def make_chunk(chunk):
         load(chunk).wait()
@@ -122,13 +122,6 @@
         edges[:, chunk_rows(chunk), :] = planes[:, :CHUNK, :].astype(jnp.bfloat16)
 
     def send_part(group, first, size):
-        def far(step, carry):
-            for turn in range(1, halves):
-                right_copy(group, first, size, turn, *partner(step)).start()
-            return carry
-
-        lax.fori_loop(0, members, far, 0)
-
         def near(step, carry):
             to_spot, to_col = partner(step)
             left_copy(group, first, size, to_spot, to_col).start()
@@ -136,6 +129,13 @@
             return carry
 
         lax.fori_loop(1, members, near, 0)
+
+        def far(step, carry):
+            for turn in range(1, halves):
+                right_copy(group, first, size, turn, *partner(step)).start()
+            return carry
+
+        lax.fori_loop(0, members, far, 0)
 
     def send_chunk(chunk):
         send_part(0, pl.multiple_of(chunk * CHUNK, CHUNK), CHUNK)

time: 139 us -> 132 us (0.950)
  Pallas kernels: 136 us -> 129 us
    pallas_call x1, Pallas kernels: 136 us -> 129 us  [fused(): pl.pallas_call(functools.partial(kernel, rows_n, ka_n, halves, groups), o...]
where the time goes in v3:
time: 132 us
  Pallas kernels  129 us (98%)
  local copies, waits for them, and re-layouts  3.16 us (2%)
    pallas_call x1, Pallas kernels, fused(): pl.pallas_call(functools.partial(kernel, rows_n, ka_n, halves, groups), o...  129 us
    unnamed x1, local copies, waits for them, and re-layouts  3.16 us

profile of v3, /device:TPU:17, one launch (start us, length us, event | category | flops | bytes accessed | tf_op | source)
XLA Modules:
  0.0 131.7 jit_solution(222926772038774210)
XLA Ops:
  0.0 128.5 %shard_map.100 = bf16[64,128,128]{2,1,0:T(8,128)(2,1)} custom-call(bf16[64,128,128]{2,1,0:T(8,128)(2,1)} %pair_hbm.1, s32[64,128]{1,0:T(8,128)} %mask_ref.1, f32[1,128]{1,0:T(1,128)} %bitcast.4, f32[1,128]{1,0:T(1,128)} %bitcast.5, bf16[128,256]{1,0:T(8,128)(2,1)} %w_proj_ref.1, bf16[128,256]{1,0:T(8,128)(2,1)} %w_gate_ref.1, ...), custom_call_target="tpu_custom_call" | custom-call | tf_op jit(solution)/shard_map/pallas_call | solution.py:270
  128.5 3.2 %copy.12 = bf16[64,128,128]{2,1,0:T(8,128)(2,1)} copy(bf16[64,128,128]{2,1,0:T(8,128)(2,1)} %shard_map.100) | data formatting | bytes 4194304
